TPU v7x, 16 devices: a 4x2x1 block of a 4x4x8 slice. The times are simulated.
16 devices in a mesh: dp: 2 (over y, z), sp: 8 (over x, core).
Axes of the slice: x: 4, y: 2, z: 1, core: 2. Of those that a mesh axis runs over, the one named last changes fastest.
The devices are a block of a 4x4x8 slice.
Arguments:
- images: float32 [12, 448, 448, 3], P('dp', 'sp'), parts along dimension 0
- w_patch: bfloat16 [14, 14, 3, 1152], replicated
- b_patch: float32 [1152], replicated
- pos_embed: bfloat16 [1024, 1152], P('sp')
- ln1_gain: float32 [1152], replicated
- ln1_bias: float32 [1152], replicated
- w_qkv: bfloat16 [1152, 3, 16, 72], replicated
- b_qkv: float32 [3, 16, 72], replicated
- w_out: bfloat16 [16, 72, 1152], replicated
- b_out: float32 [1152], replicated
- ln2_gain: float32 [1152], replicated
- ln2_bias: float32 [1152], replicated
- w_fc1: bfloat16 [1152, 4304], replicated
- b_fc1: float32 [4304], replicated
- w_fc2: bfloat16 [4304, 1152], replicated
- b_fc2: float32 [1152], replicated
Outputs:
- output: bfloat16 [12, 1024, 1152], P('dp', 'sp'), parts along dimension 0
There are 2 independent parts. A program takes and returns all parts, laid end to end along the dimension named above; an argument that names none is the same for every part.
All inputs are finite; a program needn't handle non-finite values.
Results may differ from a plain program's by a relative error of at most 0.0083589.
Values are sent between devices in bfloat16 or wider.
A program may use at most 768 MiB of HBM per device.

v0:
```python
import math
import jax
import jax.numpy as jnp
from jax import lax
from jax.sharding import PartitionSpec as P

LN_EPS = 1e-6


def layer_norm(x_in, ln_gain, ln_bias):
    row_mean = jnp.mean(x_in, axis=-1, keepdims=True)
    centered = x_in - row_mean
    variance = jnp.mean(centered * centered, axis=-1, keepdims=True)
    return centered * lax.rsqrt(variance + LN_EPS) * ln_gain + ln_bias


def embed_tokens(images, w_patch, b_patch, pos_embed):
    num_images, num_rows, num_cols, channels = images.shape
    patch_len = w_patch.shape[0]
    grid_rows = num_rows // patch_len
    grid_cols = num_cols // patch_len
    pixels = images.astype(jnp.bfloat16).reshape(num_images, grid_rows, patch_len, grid_cols, patch_len, channels)
    patch_embed = jnp.einsum('bypxqc,pqcd->byxd', pixels, w_patch, preferred_element_type=jnp.float32)
    patch_embed = patch_embed.reshape(num_images, grid_rows * grid_cols, w_patch.shape[3])
    return (patch_embed + b_patch + pos_embed.astype(jnp.float32)).astype(jnp.bfloat16)


def attend(queries, keys_all, values_all):
    num_images, n_query, num_heads, head_dim = queries.shape
    tile_len = math.gcd(n_query, 128)
    score_scale = head_dim ** -0.5

    def one_image(operands):
        q_img, k_img, v_img = operands

        def one_group(q_group):
            scores = jnp.einsum('qhe,khe->hqk', q_group, k_img, preferred_element_type=jnp.float32) * score_scale
            att_weights = jax.nn.softmax(scores, axis=-1).astype(jnp.bfloat16)
            return jnp.einsum('hqk,khe->qhe', att_weights, v_img, preferred_element_type=jnp.float32).astype(jnp.bfloat16)

        grouped = lax.map(one_group, q_img.reshape(n_query // tile_len, tile_len, num_heads, head_dim))
        return grouped.reshape(n_query, num_heads, head_dim)

    return lax.map(one_image, (queries, keys_all, values_all))


def finish_layer(x_zero, attended, w_out, b_out, ln2_gain, ln2_bias, w_fc1, b_fc1, w_fc2, b_fc2):
    residual = x_zero.astype(jnp.float32) + jnp.einsum('bnhe,hed->bnd', attended, w_out, preferred_element_type=jnp.float32) + b_out
    normed_two = layer_norm(residual, ln2_gain, ln2_bias).astype(jnp.bfloat16)
    hidden = jax.nn.gelu(jnp.einsum('bnd,df->bnf', normed_two, w_fc1, preferred_element_type=jnp.float32) + b_fc1, approximate=True).astype(jnp.bfloat16)
    return (residual + jnp.einsum('bnf,fd->bnd', hidden, w_fc2, preferred_element_type=jnp.float32) + b_fc2).astype(jnp.bfloat16)


def solution(mesh):
    def device_step(images, w_patch, b_patch, pos_embed, ln1_gain, ln1_bias, w_qkv, b_qkv, w_out, b_out, ln2_gain, ln2_bias, w_fc1, b_fc1, w_fc2, b_fc2):
        x_zero = embed_tokens(images, w_patch, b_patch, pos_embed)
        normed = layer_norm(x_zero.astype(jnp.float32), ln1_gain, ln1_bias).astype(jnp.bfloat16)
        qkv_proj = (jnp.einsum('bnd,dthe->bnthe', normed, w_qkv, preferred_element_type=jnp.float32) + b_qkv).astype(jnp.bfloat16)
        key_value = lax.all_gather(qkv_proj[:, :, 1:], 'sp', axis=1, tiled=True)
        attended = attend(qkv_proj[:, :, 0], key_value[:, :, 0], key_value[:, :, 1])
        return finish_layer(x_zero, attended, w_out, b_out, ln2_gain, ln2_bias, w_fc1, b_fc1, w_fc2, b_fc2)

    in_specs = (P('dp', 'sp', None, None), P(), P(), P('sp', None), P(), P(), P(), P(), P(), P(), P(), P(), P(), P(), P(), P())
    return jax.shard_map(device_step, mesh=mesh, in_specs=in_specs, out_specs=P('dp', 'sp', None), check_vma=False)
```

profile of v0, /device:TPU:113, one launch (start us, length us, event | category | flops | bytes accessed | tf_op | source)
XLA Modules:
  0.0 416.6 jit_solution(2857466339676863888)
XLA Ops:
  6.6 1.2 convert_element_type.40
  7.7 2.7 convert_element_type.39
  10.4 21.5 %reshape.43 = bf16[6,4,14,32,14,3]{4,3,2,1,5,0:T(8,128)(2,1)} reshape(bf16[6,56,448,3]{2,1,3,0:T(8,128)(2,1)} %convert_element_type.39) | data formatting | bytes 1806336 | tf_op jit(solution)/shard_map/reshape | solution.py:22
  31.9 12.4 %copy.27 = bf16[6,4,32,3,14,14]{2,1,5,4,0,3:T(4,128)(2,1)} copy(bf16[6,4,32,3,14,14]{5,2,4,1,3,0:T(8,128)(2,1)} %bitcast.96) | data formatting | bytes 1806336 | tf_op jit(solution)/shard_map/bypxqc,pqcd->byxd/dot_general | solution.py:23
  44.3 5.7 %reshape.52 = bf16[6,128,3,14,14]{1,4,3,0,2:T(8,128)(2,1)} reshape(bf16[6,4,32,3,14,14]{2,1,5,4,0,3:T(4,128)(2,1)} %copy.27) | data formatting | bytes 1806336 | tf_op jit(solution)/shard_map/bypxqc,pqcd->byxd/dot_general | solution.py:23
  50.0 0.0 copy-start.10
  50.0 3.6 convert_reduce_fusion
  53.6 0.6 fusion.59
  54.3 0.6 copy-done.3
  54.8 9.9 %add_convert_fusion = bf16[6,128,3,16,72]{1,4,3,2,0:T(8,128)(2,1)S(1)} fusion(f32[3,16,72]{2,1,0:T(8,128)S(1)} %copy-done.6, bf16[1152,3,16,72]{0,3,2,1:T(8,128)(2,1)} %param.24, bf16[6,128,1152]{2,1,0:T(8,128)(2,1)S(1)} %get-tuple-element.61, f32[1152]{0:T(1024)S(1)} %copy-done.9, f32[1152]{0:T(1024)S(1)} %copy-done.10, f32[6,128]{1,0:T(8,128)S(1)} %add_rsqrt_fusion.1, ...), kind=kOutput, calls=%fused_computation.33 | convolution fusion | flops 6125912064 | bytes 15069696 | tf_op jit(solution)/shard_map/bnd,dthe->bnthe/dot_general | solution.py:58
  64.8 2.3 copy-done.4
  67.1 2.4 slice.16
  69.4 0.1 all-gather.2.cloned.1.call-update
  69.5 2.8 slice_bitcast_fusion.2
  72.3 136.8 %all-gather.2.cloned.1.call-done = bf16[6,1024,2,16,72]{1,4,3,2,0:T(8,128)(2,1)} async-done(((bf16[6,128,2,16,72]{1,4,3,2,0:T(8,128)(2,1)}), bf16[6,1024,2,16,72]{1,4,3,2,0:T(8,128)(2,1)}) %all-gather.2.cloned.1.call-update) | async-done | bytes 28311568 | tf_op jit(solution)/shard_map/all_gather | solution.py:59
  209.1 20.7 %slice_bitcast_fusion = (bf16[6,1024,16,72]{1,3,2,0:T(8,128)(2,1)}, bf16[6,1024,16,72]{1,3,2,0:T(8,128)(2,1)}) fusion(bf16[6,1024,2,16,72]{1,4,3,2,0:T(8,128)(2,1)} %all-gather.2.cloned.1.call-done), kind=kLoop, calls=%fused_computation.23 | loop fusion | bytes 56623104 | tf_op jit(solution)/shard_map/squeeze | solution.py:60
  229.8 130.2 %while.10 = (s32[]{:T(128)}, bf16[6,128,16,72]{1,3,2,0:T(8,128)(2,1)}, bf16[6,1024,16,72]{1,3,2,0:T(8,128)(2,1)}, bf16[6,128,16,72]{1,3,2,0:T(8,128)(2,1)}, bf16[6,1024,16,72]{1,3,2,0:T(8,128)(2,1)}, /*index=5*/s32[]{:T(128)}) while((s32[]{:T(128)}, bf16[6,128,16,72]{1,3,2,0:T(8,128)(2,1)}, bf16[6,1024,16,72]{1,3,2,0:T(8,128)(2,1)}, ...), condition=%wide.region_5.6_spmd, body=%wide.region_2.5_spmd.sunk | while | flops 623005696 | bytes 72435816 | solution.py:44
  242.1 3.1 fusion.107
  245.1 3.2 copy-done.1
  248.3 2.3 fusion.108
  250.6 11.1 %fusion.109 = bf16[6,128,16,72]{1,3,2,0:T(8,128)(2,1)} fusion(bf16[6,128,16,72]{1,3,2,0:T(8,128)(2,1)} %get-tuple-element.102, s32[]{:T(128)S(6)} %copy.38, f32[16,128]{1,0:T(8,128)S(1)} %fusion.108, bf16[6,1024,16,72]{1,3,2,0:T(8,128)(2,1)} %get-tuple-element.109, f32[16,128,1024]{2,1,0:T(8,128)} %copy-done.1), kind=kOutput, calls=%fused_computation.14.clone.1 | convolution fusion | flops 312626176 | bytes 19440640 | tf_op jit(solution)/shard_map/while/body/eval_jaxpr/while/body/eval_jaxpr/hqk,khe->qhe/dot_general | solution.py:39
  261.7 3.1 fusion.107
  264.8 3.2 copy-done.1
  268.0 2.3 fusion.108
  270.3 11.1 %fusion.109 = bf16[6,128,16,72]{1,3,2,0:T(8,128)(2,1)} fusion(bf16[6,128,16,72]{1,3,2,0:T(8,128)(2,1)} %get-tuple-element.102, s32[]{:T(128)S(6)} %copy.38, f32[16,128]{1,0:T(8,128)S(1)} %fusion.108, bf16[6,1024,16,72]{1,3,2,0:T(8,128)(2,1)} %get-tuple-element.109, f32[16,128,1024]{2,1,0:T(8,128)} %copy-done.1), kind=kOutput, calls=%fused_computation.14.clone.1 | convolution fusion | flops 312626176 | bytes 19440640 | tf_op jit(solution)/shard_map/while/body/eval_jaxpr/while/body/eval_jaxpr/hqk,khe->qhe/dot_general | solution.py:39
  281.4 3.1 fusion.107
  284.5 3.2 copy-done.1
  287.7 2.3 fusion.108
  290.0 11.1 %fusion.109 = bf16[6,128,16,72]{1,3,2,0:T(8,128)(2,1)} fusion(bf16[6,128,16,72]{1,3,2,0:T(8,128)(2,1)} %get-tuple-element.102, s32[]{:T(128)S(6)} %copy.38, f32[16,128]{1,0:T(8,128)S(1)} %fusion.108, bf16[6,1024,16,72]{1,3,2,0:T(8,128)(2,1)} %get-tuple-element.109, f32[16,128,1024]{2,1,0:T(8,128)} %copy-done.1), kind=kOutput, calls=%fused_computation.14.clone.1 | convolution fusion | flops 312626176 | bytes 19440640 | tf_op jit(solution)/shard_map/while/body/eval_jaxpr/while/body/eval_jaxpr/hqk,khe->qhe/dot_general | solution.py:39
  301.1 3.1 fusion.107
  304.2 3.2 copy-done.1
  307.4 2.3 fusion.108
  309.7 11.1 %fusion.109 = bf16[6,128,16,72]{1,3,2,0:T(8,128)(2,1)} fusion(bf16[6,128,16,72]{1,3,2,0:T(8,128)(2,1)} %get-tuple-element.102, s32[]{:T(128)S(6)} %copy.38, f32[16,128]{1,0:T(8,128)S(1)} %fusion.108, bf16[6,1024,16,72]{1,3,2,0:T(8,128)(2,1)} %get-tuple-element.109, f32[16,128,1024]{2,1,0:T(8,128)} %copy-done.1), kind=kOutput, calls=%fused_computation.14.clone.1 | convolution fusion | flops 312626176 | bytes 19440640 | tf_op jit(solution)/shard_map/while/body/eval_jaxpr/while/body/eval_jaxpr/hqk,khe->qhe/dot_general | solution.py:39
  320.7 3.1 fusion.107
  323.8 3.2 copy-done.1
  327.0 2.3 fusion.108
  329.3 11.1 %fusion.109 = bf16[6,128,16,72]{1,3,2,0:T(8,128)(2,1)} fusion(bf16[6,128,16,72]{1,3,2,0:T(8,128)(2,1)} %get-tuple-element.102, s32[]{:T(128)S(6)} %copy.38, f32[16,128]{1,0:T(8,128)S(1)} %fusion.108, bf16[6,1024,16,72]{1,3,2,0:T(8,128)(2,1)} %get-tuple-element.109, f32[16,128,1024]{2,1,0:T(8,128)} %copy-done.1), kind=kOutput, calls=%fused_computation.14.clone.1 | convolution fusion | flops 312626176 | bytes 19440640 | tf_op jit(solution)/shard_map/while/body/eval_jaxpr/while/body/eval_jaxpr/hqk,khe->qhe/dot_general | solution.py:39
  340.4 3.1 fusion.107
  343.5 3.2 copy-done.1
  346.7 2.3 fusion.108
  349.0 11.1 %fusion.109 = bf16[6,128,16,72]{1,3,2,0:T(8,128)(2,1)} fusion(bf16[6,128,16,72]{1,3,2,0:T(8,128)(2,1)} %get-tuple-element.102, s32[]{:T(128)S(6)} %copy.38, f32[16,128]{1,0:T(8,128)S(1)} %fusion.108, bf16[6,1024,16,72]{1,3,2,0:T(8,128)(2,1)} %get-tuple-element.109, f32[16,128,1024]{2,1,0:T(8,128)} %copy-done.1), kind=kOutput, calls=%fused_computation.14.clone.1 | convolution fusion | flops 312626176 | bytes 19440640 | tf_op jit(solution)/shard_map/while/body/eval_jaxpr/while/body/eval_jaxpr/hqk,khe->qhe/dot_general | solution.py:39
  360.1 5.1 %fusion.92 = (f32[6,128]{1,0:T(8,128)S(1)}, f32[6,128,1152]{2,1,0:T(8,128)S(1)}) fusion(f32[1152]{0:T(1024)S(1)} %copy-done.5, bf16[6,128,16,72]{1,3,2,0:T(8,128)(2,1)} %get-tuple-element.47, bf16[16,72,1152]{2,1,0:T(8,128)(2,1)S(1)} %copy-done, bf16[6,128,1152]{2,1,0:T(8,128)(2,1)} %copy-done.3), kind=kOutput, calls=%fused_computation.81 | convolution fusion | flops 2041969920 | bytes 9739776 | tf_op jit(solution)/shard_map/bnhe,hed->bnd/dot_general | solution.py:48
  365.2 0.0 copy-start.7
  365.2 0.0 copy-start.11
  365.2 0.0 copy-start.12
  365.3 1.7 copy-done.2
  367.0 0.5 multiply_reduce_fusion.1
  367.5 42.1 %fusion.63 = bf16[6,128,1152]{2,1,0:T(8,128)(2,1)} fusion(f32[6,128,1152]{2,1,0:T(8,128)} %copy-done.2, bf16[4304,1152]{1,0:T(8,128)(2,1)} %param.32, bf16[1152,4304]{0,1:T(8,128)(2,1)} %param.30, f32[4304]{0:T(1024)S(1)} %copy-done.7, f32[1152]{0:T(1024)S(1)} %copy-done.11, f32[1152]{0:T(1024)S(1)} %copy-done.12, f32[1152]{0:T(1024)S(1)} %copy-done.13, ...), kind=kOutput, calls=%fused_computation.58 | convolution fusion | flops 15271747584 | bytes 25178432 | tf_op jit(solution)/shard_map/bnf,fd->bnd/dot_general | solution.py:51
  (31 shorter events, 0.1 us)
Async XLA Ops:
  6.5 353.5 %copy-start = (bf16[16,72,1152]{2,1,0:T(8,128)(2,1)S(1)}, bf16[16,72,1152]{2,1,0:T(8,128)(2,1)}, u32[]{:S(2)}) copy-start(bf16[16,72,1152]{2,1,0:T(8,128)(2,1)} %param.26) | copy-start | bytes 7962628
  6.6 202.6 %all-gather.2.cloned.1.call-start = ((), (), s32[]{:S(2)}) async-start(), calls=%async_computation | async-start | bytes 31850496 | tf_op jit(solution)/shard_map/all_gather | solution.py:59
  44.3 5.7 %copy-start.8 = (f32[1152]{0:T(1024)S(1)}, f32[1152]{0:T(1024)}, u32[]{:S(2)}) copy-start(f32[1152]{0:T(1024)} %param.20) | copy-start | bytes 13828
  50.0 4.8 %copy-start.6 = (f32[3,16,72]{2,1,0:T(8,128)S(1)}, f32[3,16,72]{2,1,0:T(8,128)}, u32[]{:S(2)}) copy-start(f32[3,16,72]{2,1,0:T(8,128)} %param.25) | copy-start | bytes 41476
  50.0 4.8 %copy-start.9 = (f32[1152]{0:T(1024)S(1)}, f32[1152]{0:T(1024)}, u32[]{:S(2)}) copy-start(f32[1152]{0:T(1024)} %param.23) | copy-start | bytes 13828
  50.0 4.8 %copy-start.10 = (f32[1152]{0:T(1024)S(1)}, f32[1152]{0:T(1024)}, u32[]{:S(2)}) copy-start(f32[1152]{0:T(1024)} %param.22) | copy-start | bytes 13828
  53.6 1.2 copy-start.3
  64.8 2.3 copy-start.4
  229.8 130.2 %copy-start.5 = (f32[1152]{0:T(1024)S(1)}, f32[1152]{0:T(1024)}, u32[]{:S(2)}) copy-start(f32[1152]{0:T(1024)} %param.27) | copy-start | bytes 13828
  245.1 3.2 copy-start.1
  264.8 3.2 copy-start.1
  284.5 3.2 copy-start.1
  304.1 3.2 copy-start.1
  323.8 3.2 copy-start.1
  343.5 3.2 copy-start.1
  365.2 1.8 copy-start.2
  365.2 2.3 copy-start.7
  365.2 2.2 copy-start.11
  365.2 2.2 copy-start.12
  365.3 2.2 copy-start.13
Sparse Core Ops, SparseCore 0:
  69.6 139.4 all-gather.1
where the time goes:
time: 424 us; the launch traced here: 417 us
  matrix products  146 us (34%)
  waiting for transfers between devices  137 us (32%)
  local copies, waits for them, and re-layouts  89.4 us (21%)
  other arithmetic  18.7 us (4%)
  between operations  13.8 us (3%)
  loops' own time  12.4 us (3%)
    all_gather x1, waiting for transfers between devices, device_step(): key_value = lax.all_gather(qkv_proj[:, :, 1:], 'sp', axis=1, tiled=True)  137 us
    dot_general x6, matrix products, one_group(): jnp.einsum('hqk,khe->qhe', att_weights, v_img, preferred_element_type=jnp...  66.5 us
    dot_general x1, matrix products, finish_layer(): jnp.einsum('bnf,fd->bnd', hidden, w_fc2, preferred_element_type=jnp.float32)  42.1 us
    squeeze x2, local copies, waits for them, and re-layouts, device_step(): attended = attend(qkv_proj[:, :, 0], key_value[:, :, 0], key_value[:, :, 1])  23.6 us
    reshape x1, local copies, waits for them, and re-layouts, embed_tokens(): images.astype(jnp.bfloat16)  21.5 us
    while x12, local copies, waits for them, and re-layouts  19.3 us
    dot_general x6, matrix products, one_group(): jnp.einsum('qhe,khe->hqk', q_group, k_img, preferred_element_type=jnp.flo...  18.4 us
    dot_general x2, local copies, waits for them, and re-layouts, embed_tokens(): jnp.einsum('bypxqc,pqcd->byxd', pixels, w_patch, preferred_element_type=j...  18.1 us
  transfers between devices with their start and end apart: 1, of which 1 were waited for; matrix products, arithmetic and copies ran while one was open for 1% of the time, Pallas kernels for 0%

commit v1 on v0

v1 whole, which is shorter than its diff:
```python
import functools
import math
import jax
import jax.numpy as jnp
from jax import lax
from jax.experimental import pallas as pl
from jax.experimental.pallas import tpu as pltpu
from jax.sharding import PartitionSpec as P

LN_EPS = 1e-6
MESH = pl.DeviceIdType.MESH
F32 = jnp.float32
BF16 = jnp.bfloat16


def layer_norm(x_in, ln_gain, ln_bias):
    row_mean = jnp.mean(x_in, axis=-1, keepdims=True)
    centered = x_in - row_mean
    variance = jnp.mean(centered * centered, axis=-1, keepdims=True)
    return centered * lax.rsqrt(variance + LN_EPS) * ln_gain + ln_bias


def embed_tokens(images, w_patch, b_patch, pos_embed):
    num_images, num_rows, num_cols, channels = images.shape
    patch_len = w_patch.shape[0]
    patch_embed = lax.conv_general_dilated(
        images.astype(BF16), w_patch, (patch_len, patch_len), 'VALID',
        dimension_numbers=('NHWC', 'HWIO', 'NHWC'), preferred_element_type=F32)
    patch_embed = patch_embed.reshape(num_images, -1, w_patch.shape[3])
    return (patch_embed + b_patch + pos_embed.astype(F32)).astype(BF16)


def attend_kernel(n_chip, scale, y_ref, bias_ref, w_hbm, o_out,
                  y_b, y_a, w_b, w_a, q_b, k_b, v_b, q_a, k_a, v_a, s_buf, m_buf, o_b, o_a,
                  w_sem, y_send, y_recv, f_send, f_recv, o_send, o_recv):
    me = lax.axis_index('sp')
    chip = me // 2
    core = lax.rem(me, 2)
    sib = chip * 2 + (1 - core)
    heads_b, heads_a = w_b.shape[1] // 72, w_a.shape[1] // 72
    dim = y_ref.shape[2]
    n_dev = 2 * n_chip
    odd = lax.rem(chip, 2)
    half = chip // 2

    def image_of(owner, unit):
        first = (owner // 2) * 3
        return first + 1 if unit == 0 else first + 2 * lax.rem(owner, 2)

    head_b = (odd * 2 + core) * heads_b
    head_a = core * heads_a

    w_copies = []
    for t in range(3):
        for u, (w_s, h0) in enumerate(((w_b, head_b), (w_a, head_a))):
            rows = w_s.shape[1]
            c = pltpu.make_async_copy(
                w_hbm.at[pl.ds(pl.multiple_of(t * dim + h0 * 72, 8), rows)], w_s.at[t], w_sem.at[u, t])
            c.start()
            w_copies.append((u, c))

    barrier = pltpu.get_barrier_semaphore()
    for j in range(1, n_dev):
        pl.semaphore_signal(barrier, inc=1, device_id={'sp': lax.rem(me + j, n_dev)}, device_id_type=MESH)
    pl.semaphore_wait(barrier, n_dev - 1)

    offs = (0, 1, 3, 2)
    back = {0: 0, 1: 2, 2: 1, 3: 3}
    y_units = (y_b, y_a)
    sends = []
    for u in range(2):
        for j in range(1, n_chip):
            owner = lax.rem(chip + offs[j], n_chip)
            dst = y_units[u].at[back[j], core]
            c = pltpu.make_async_remote_copy(
                y_ref.at[image_of(owner, u)], dst, y_send.at[u, j], y_recv.at[u, back[j]],
                device_id={'sp': owner * 2 + core}, device_id_type=MESH)
            c.start()
            sends.append(c)
    forwards = {}
    for u in range(2):
        c = pltpu.make_async_remote_copy(
            y_ref.at[image_of(chip, u)], y_units[u].at[0, core], f_send.at[u, 0], f_recv.at[u, 0],
            device_id={'sp': sib}, device_id_type=MESH)
        c.start()
        forwards[u, 0] = c
    for u in range(2):
        y_units[u][0, core] = y_ref[image_of(chip, u)]

    def recv_copy(u, j):
        return pltpu.make_async_remote_copy(
            y_ref.at[0], y_units[u].at[j, core], y_send.at[u, 1], y_recv.at[u, j],
            device_id={'sp': sib}, device_id_type=MESH)

    def project(u, j):
        y_u = y_units[u]
        w_u = (w_b, w_a)[u]
        qkv = ((q_b, k_b, v_b), (q_a, k_a, v_a))[u]
        heads = (heads_b, heads_a)[u]
        h0 = (head_b, head_a)[u]
        y_chunk = y_u[j].reshape(256, dim)
        step = 4
        for t in range(3):
            for g in range(0, heads, step):
                prod = lax.dot_general(w_u[t, g * 72:(g + step) * 72], y_chunk, (((1,), (1,)), ((), ())),
                                       preferred_element_type=F32)
                for h in range(step):
                    row0 = pl.multiple_of(t * dim + (h0 + g + h) * 72, 8)
                    val = prod[h * 72:(h + 1) * 72] + bias_ref[pl.ds(row0, 72)]
                    if t == 1:
                        qkv[t][g + h, 256 * j:256 * (j + 1), :] = val.T.astype(BF16)
                    else:
                        qkv[t][g + h, :, 256 * j:256 * (j + 1)] = val.astype(BF16)

    def scores(u, item, slot):
        q_u, k_u = ((q_b, k_b), (q_a, k_a))[u]
        h = item // n_chip
        blk = pl.ds(pl.multiple_of(lax.rem(item, n_chip) * 256, 256), 256)
        s = jnp.dot(k_u[h], q_u[h, :, blk], preferred_element_type=F32)
        s_buf[slot] = s
        m_buf[slot] = jnp.broadcast_to(jnp.max(s, axis=0, keepdims=True), (8, 256))

    def weigh(u, item, slot):
        v_u = (v_b, v_a)[u]
        o_u = (o_b, o_a)[u]
        h = item // n_chip
        j = lax.rem(item, n_chip)
        e = jnp.exp2((s_buf[slot] - m_buf[slot][:1]) * scale)
        total = jnp.sum(e, axis=0, keepdims=True)
        o = jnp.dot(v_u[h], e.astype(BF16), preferred_element_type=F32) * (1.0 / total)
        o = o.astype(BF16)
        o_u[j, 0, h] = o[:, :128]
        o_u[j, 1, h] = o[:, 128:]

    def attend(u, first, last):
        scores(u, first, 0)

        def body(i, carry):
            item = first + 2 * i
            scores(u, item + 1, 1)
            weigh(u, item, 0)
            scores(u, lax.min(item + 2, last - 1), 0)
            weigh(u, item + 1, 1)
            return carry

        lax.fori_loop(0, (last - first) // 2, body, 0)

    out_sends = []

    def send_out(u, g, g0, heads_out):
        o_u = (o_b, o_a)[u]
        h0 = (head_b, head_a)[u]
        for j in range(n_chip):
            owner = lax.rem(chip + offs[j], n_chip)
            for c2 in range(2):
                dst_core = core if c2 == 0 else 1 - core
                src = o_u.at[j, dst_core, pl.ds(g0, heads_out)]
                dst = o_out.at[image_of(chip, u), pl.ds(h0 + g0, heads_out)]
                if j == 0 and c2 == 0:
                    c = pltpu.make_async_copy(src, dst, o_recv.at[g, 0, 0])
                else:
                    c = pltpu.make_async_remote_copy(
                        src, dst, o_send.at[g, j, c2], o_recv.at[g, back[j], c2],
                        device_id={'sp': owner * 2 + dst_core}, device_id_type=MESH)
                c.start()
                out_sends.append((c, j == 0 and c2 == 0))

    for u in range(2):
        for uu, c in w_copies:
            if uu == u:
                c.wait()
        for j in range(n_chip):
            if j > 0:
                recv_copy(u, j).wait_recv()
                f = pltpu.make_async_remote_copy(
                    y_units[u].at[j, core], y_units[u].at[j, core], f_send.at[u, j], f_recv.at[u, j],
                    device_id={'sp': sib}, device_id_type=MESH)
                f.start()
                forwards[u, j] = f
            pltpu.make_async_remote_copy(
                y_units[u].at[j, core], y_units[u].at[j, 1 - core], f_send.at[u, j], f_recv.at[u, j],
                device_id={'sp': sib}, device_id_type=MESH).wait_recv()
            project(u, j)
        if u == 0:
            attend(u, 0, heads_b * n_chip)
            send_out(u, 0, 0, heads_b)
        else:
            attend(u, 0, heads_b * n_chip)
            send_out(u, 1, 0, heads_b)
            attend(u, heads_b * n_chip, heads_a * n_chip)
            send_out(u, 2, heads_b, heads_a - heads_b)

    for c in sends:
        c.wait_send()
    for c in forwards.values():
        c.wait_send()
    for c, local in out_sends:
        if local:
            c.wait()
        else:
            c.wait_send()
    for g in range(3):
        u = 0 if g == 0 else 1
        nh = heads_b if g < 2 else heads_a - heads_b
        for j in range(n_chip):
            for c2 in range(2):
                if j == 0 and c2 == 0:
                    continue
                src_chip = lax.rem(chip + offs[j], n_chip)
                src_core = core if c2 == 0 else 1 - core
                if u == 0:
                    h_src = (lax.rem(src_chip, 2) * 2 + src_core) * heads_b
                else:
                    h_src = src_core * heads_a + (0 if g == 1 else heads_b)
                pltpu.make_async_remote_copy(
                    (o_b, o_a)[u].at[0, 0, pl.ds(0, nh)], o_out.at[image_of(src_chip, u), pl.ds(h_src, nh)],
                    o_send.at[g, j, c2], o_recv.at[g, j, c2],
                    device_id={'sp': sib}, device_id_type=MESH).wait_recv()


def attend_layer(normed, w_qkv_t, bias_col, n_dev, num_heads, head_dim):
    images, band, dim = normed.shape
    n_chip = n_dev // 2
    heads_b, heads_a = num_heads // 4, num_heads // 2
    keys = band * n_dev
    scale = head_dim ** -0.5 * math.log2(math.e)

    def unit(heads):
        return [pltpu.VMEM((heads, head_dim, keys), BF16), pltpu.VMEM((heads, keys, head_dim), BF16),
                pltpu.VMEM((heads, head_dim, keys), BF16)]

    vmem = pl.BlockSpec(memory_space=pltpu.VMEM)
    hbm = pl.BlockSpec(memory_space=pl.ANY)
    dma = pltpu.SemaphoreType.DMA
    return pl.pallas_call(
        functools.partial(attend_kernel, n_chip, scale),
        out_shape=jax.ShapeDtypeStruct((images, num_heads, head_dim, band), BF16),
        in_specs=[vmem, vmem, hbm],
        out_specs=hbm,
        scratch_shapes=[
            pltpu.VMEM((n_chip, 2, band, dim), BF16), pltpu.VMEM((n_chip, 2, band, dim), BF16),
            pltpu.VMEM((3, heads_b * head_dim, dim), BF16), pltpu.VMEM((3, heads_a * head_dim, dim), BF16),
            *unit(heads_b), *unit(heads_a),
            pltpu.VMEM((2, keys, 256), F32), pltpu.VMEM((2, 8, 256), F32),
            pltpu.VMEM((n_chip, 2, heads_b, head_dim, band), BF16),
            pltpu.VMEM((n_chip, 2, heads_a, head_dim, band), BF16),
            dma((2, 3)), dma((2, n_chip)), dma((2, n_chip)), dma((2, n_chip)), dma((2, n_chip)),
            dma((3, n_chip, 2)), dma((3, n_chip, 2)),
        ],
        compiler_params=pltpu.CompilerParams(collective_id=0, has_side_effects=True, vmem_limit_bytes=50 * 2**20),
        name='attend',
    )(normed, bias_col, w_qkv_t)


def mlp_kernel(chunk, tail, o_ref, x_ref, wo_ref, bo_ref, g2_ref, c2_ref, b1_ref, b2_ref, w1_hbm, w2_hbm, out_ref,
               w1, w2, acc, y2, hid, sem1, sem2):
    n_full = (w1.shape[0] - tail) // chunk

    def w_copy(i, size):
        rows = pl.ds(i * chunk, size) if isinstance(i, int) else pl.ds(pl.multiple_of(i * chunk, chunk), size)
        return (pltpu.make_async_copy(w1_hbm.at[rows], w1.at[rows], sem1.at[i]),
                pltpu.make_async_copy(w2_hbm.at[rows], w2.at[rows], sem2.at[i]))

    for i in range(n_full + 1):
        for c in w_copy(i, chunk if i < n_full else tail):
            c.start()
    n_img, band = o_ref.shape[0], o_ref.shape[2]

    def proj(i, carry):
        rows = pl.ds(pl.multiple_of(i * band, band), band)
        r = lax.dot_general(o_ref[i], wo_ref[...], (((0,), (0,)), ((), ())), preferred_element_type=F32)
        r = x_ref[rows].astype(F32) + r + bo_ref[...]
        acc[rows] = r + b2_ref[...]
        y2[rows] = layer_norm(r, g2_ref[...], c2_ref[...]).astype(BF16)
        return carry

    lax.fori_loop(0, n_img, proj, 0)

    def first(i, size, slot):
        rows = pl.ds(i * chunk, size) if isinstance(i, int) else pl.ds(pl.multiple_of(i * chunk, chunk), size)
        pre = lax.dot_general(y2[...], w1[rows], (((1,), (1,)), ((), ())), preferred_element_type=F32)
        pre = pre + b1_ref[:, rows]
        hid[slot, :, :size] = jax.nn.gelu(pre, approximate=True).astype(BF16)

    def second(i, size, slot):
        rows = pl.ds(i * chunk, size) if isinstance(i, int) else pl.ds(pl.multiple_of(i * chunk, chunk), size)
        acc[...] += jnp.dot(hid[slot, :, :size], w2[rows], preferred_element_type=F32)

    w_copy(0, chunk)[0].wait()
    first(0, chunk, 0)

    def body(i, carry):
        w_copy(i + 1, chunk)[0].wait()
        w_copy(i, chunk)[1].wait()
        first(i + 1, chunk, lax.rem(i + 1, 2))
        second(i, chunk, lax.rem(i, 2))
        return carry

    lax.fori_loop(0, n_full - 1, body, 0)
    w_copy(n_full, tail)[0].wait()
    w_copy(n_full - 1, chunk)[1].wait()
    first(n_full, tail, n_full % 2)
    second(n_full - 1, chunk, (n_full - 1) % 2)
    w_copy(n_full, tail)[1].wait()
    second(n_full, tail, n_full % 2)
    out_ref[...] = acc[...].astype(BF16)


def mlp_layer(o_t, x_zero, w_out, b_out, ln2_gain, ln2_bias, w_fc1_t, b_fc1, w_fc2, b_fc2):
    images, dim, band = o_t.shape
    ff = w_fc2.shape[0]
    rows = images * band
    chunk = 512
    tail = ff - (ff - 1) // chunk * chunk
    n_chunks = (ff - tail) // chunk + 1
    vmem = pl.BlockSpec(memory_space=pltpu.VMEM)
    hbm = pl.BlockSpec(memory_space=pl.ANY)
    flops = 2 * rows * dim * (dim + 2 * ff)
    return pl.pallas_call(
        functools.partial(mlp_kernel, chunk, tail),
        out_shape=jax.ShapeDtypeStruct((rows, dim), BF16),
        in_specs=[vmem] * 8 + [hbm, hbm],
        out_specs=vmem,
        scratch_shapes=[
            pltpu.VMEM((ff, dim), BF16), pltpu.VMEM((ff, dim), BF16), pltpu.VMEM((rows, dim), F32),
            pltpu.VMEM((rows, dim), BF16), pltpu.VMEM((2, rows, chunk), BF16),
            pltpu.SemaphoreType.DMA((n_chunks,)), pltpu.SemaphoreType.DMA((n_chunks,)),
        ],
        compiler_params=pltpu.CompilerParams(vmem_limit_bytes=56 * 2**20),
        cost_estimate=pl.CostEstimate(flops=flops, bytes_accessed=32 * 2**20, transcendentals=0),
        name='mlp',
    )(o_t, x_zero, w_out, b_out[None], ln2_gain[None], ln2_bias[None], b_fc1[None], b_fc2[None], w_fc1_t, w_fc2)


def solution(mesh):
    n_dev = mesh.shape['sp']

    def device_step(images, w_patch, b_patch, pos_embed, ln1_gain, ln1_bias, w_qkv, b_qkv, w_out, b_out, ln2_gain, ln2_bias, w_fc1, b_fc1, w_fc2, b_fc2):
        dim, _, num_heads, head_dim = w_qkv.shape
        x_zero = embed_tokens(images, w_patch, b_patch, pos_embed)
        normed = layer_norm(x_zero.astype(F32), ln1_gain, ln1_bias).astype(BF16)
        w_qkv_t = jnp.transpose(w_qkv, (1, 2, 3, 0)).reshape(3 * dim, dim)
        o_t = attend_layer(normed, w_qkv_t, b_qkv.reshape(3 * dim, 1), n_dev, num_heads, head_dim)
        num_images, band = normed.shape[:2]
        out = mlp_layer(o_t.reshape(num_images, dim, band), x_zero.reshape(num_images * band, dim), w_out.reshape(dim, dim),
                        b_out, ln2_gain, ln2_bias, w_fc1.T, b_fc1, w_fc2, b_fc2)
        return out.reshape(num_images, band, dim)

    in_specs = (P('dp', 'sp', None, None), P(), P(), P('sp', None), P(), P(), P(), P(), P(), P(), P(), P(), P(), P(), P(), P())
    return jax.shard_map(device_step, mesh=mesh, in_specs=in_specs, out_specs=P('dp', 'sp', None), check_vma=False)
```

time: 424 us -> 189 us (0.45); the launches traced: 417 us -> 189 us
  waiting for transfers between devices: 137 us -> 0 us
  matrix products: 146 us -> 49.6 us
  Pallas kernels: 0 us -> 95.6 us
  local copies, waits for them, and re-layouts: 89.4 us -> 32.1 us
  between operations: 13.8 us -> 0.31 us
  loops' own time: 12.4 us -> 0 us
  other arithmetic: 18.7 us -> 10.9 us
    dot_general x16 -> x0, matrix products: 146 us -> none  [the longest x6 66.5 us: one_group(): jnp.einsum('hqk,khe->qhe', att_weights, v_img, preferred_element_type=jnp...]
    all_gather x1 -> x0, waiting for transfers between devices: 137 us -> none  [device_step(): key_value = lax.all_gather(qkv_proj[:, :, 1:], 'sp', axis=1, tiled=True)]
    pallas_call x0 -> x2, Pallas kernels: none -> 95.6 us  [the longest x1 64 us: attend_layer(): pl.pallas_call(functools.partial(attend_kernel, n_chip, scale), out_shape...]
    conv_general_dilated x0 -> x1, matrix products: none -> 49.6 us  [embed_tokens(): lax.conv_general_dilated(images.astype(BF16), w_patch, (patch_len, patch_...]
    squeeze x2 -> x0, local copies, waits for them, and re-layouts: 23.6 us -> none  [device_step(): attended = attend(qkv_proj[:, :, 0], key_value[:, :, 0], key_value[:, :, 1])]
    convert_element_type x0 -> x1, local copies, waits for them, and re-layouts: none -> 21.1 us  [embed_tokens(): images.astype(BF16)]
    reshape x1, local copies, waits for them, and re-layouts: 21.5 us -> 1.73 us  [device_step(): b_qkv.reshape(3 * dim, 1)]
    while x12 -> x0, local copies, waits for them, and re-layouts: 19.3 us -> none
  transfers between devices with their start and end apart: 1 -> 0, of which waited for: 1 -> 0; matrix products, arithmetic and copies ran while one was open for 1% -> 0% of each run, Pallas kernels for 0% -> 0%
where the time goes in v1:
time: 189 us
  Pallas kernels  95.6 us (51%)
  matrix products  49.6 us (26%)
  local copies, waits for them, and re-layouts  32.1 us (17%)
  other arithmetic  10.9 us (6%)
    pallas_call x1, Pallas kernels, attend_layer(): pl.pallas_call(functools.partial(attend_kernel, n_chip, scale), out_shape...  64 us
    conv_general_dilated x1, matrix products, embed_tokens(): lax.conv_general_dilated(images.astype(BF16), w_patch, (patch_len, patch_...  49.6 us
    pallas_call x1, Pallas kernels, mlp_layer(): pl.pallas_call(functools.partial(mlp_kernel, chunk, tail), out_shape=jax....  31.6 us
    convert_element_type x1, local copies, waits for them, and re-layouts, embed_tokens(): images.astype(BF16)  21.1 us
    conv_general_dilated x1, local copies, waits for them, and re-layouts, embed_tokens(): lax.conv_general_dilated(images.astype(BF16), w_patch, (patch_len, patch_...  4.85 us

profile of v1, /device:TPU:113, one launch (start us, length us, event | category | flops | bytes accessed | tf_op | source)
XLA Modules:
  0.0 188.5 jit_solution(9743162319384542776)
XLA Ops:
  0.0 0.0 copy-start
  0.0 1.1 convert_element_type.27
  1.1 0.0 copy-start.4
  1.1 1.9 %convert_element_type.26 = bf16[6,56,448,3]{2,1,3,0:T(8,128)(2,1)S(1)} convert(f32[6,56,448,3]{2,1,3,0:T(8,128)} %param.16) | non-fusion elementwise | flops 451584 | bytes 2709504 | tf_op jit(solution)/shard_map/convert_element_type | solution.py:27
  3.1 0.0 copy-start.6
  3.1 21.1 %copy.36 = bf16[6,56,448,3]{0,3,2,1:T(4,128)(2,1)} copy(bf16[6,56,448,3]{2,1,3,0:T(8,128)(2,1)S(1)} %convert_element_type.26) | data formatting | bytes 1806336 | tf_op jit(solution)/shard_map/convert_element_type | solution.py:27
  24.2 0.0 copy-done
  24.2 0.0 copy-done.6
  24.2 49.6 %convert_reduce_fusion = (f32[6,4,32]{0,2,1:T(8,128)S(1)}, f32[6,4,32,1152]{3,0,2,1:T(8,128)}) fusion(f32[4,32,1152]{2,1,0:T(8,128)S(1)} %bitcast.28, f32[1152]{0:T(1024)S(1)} %copy-done.6, bf16[6,56,448,3]{0,3,2,1:T(4,128)(2,1)} %copy.36, bf16[14,14,3,1152]{3,1,2,0:T(8,128)(2,1)S(1)} %copy-done), kind=kOutput, calls=%fused_computation.1 | convolution fusion | flops 1044872448 | bytes 6394368 | tf_op jit(solution)/shard_map/conv_general_dilated | solution.py:26
  73.8 0.0 copy-done.4
  73.8 3.4 %fusion.1 = f32[6,4,32]{0,2,1:T(8,128)S(1)} fusion(f32[6,4,32]{0,2,1:T(8,128)S(1)} %broadcast_multiply_fusion, f32[4,32,1152]{2,1,0:T(8,128)S(1)} %bitcast.29, f32[6,4,32,1152]{3,0,2,1:T(8,128)} %get-tuple-element.6, f32[1152]{0:T(1024)S(1)} %copy-done.6), kind=kLoop, calls=%fused_computation.3 | loop fusion | flops 6192384 | bytes 4139520 | tf_op jit(solution)/shard_map/reduce_sum | solution.py:19
  77.3 0.1 copy.48
  77.3 0.0 copy-start.5
  77.3 0.0 copy-start.9
  77.3 0.0 copy-start.10
  77.3 4.8 %copy.38 = f32[6,4,32,1152]{3,2,1,0:T(8,128)} copy(f32[6,4,32,1152]{3,0,2,1:T(8,128)} %get-tuple-element.6) | data formatting | bytes 7077888 | tf_op jit(solution)/shard_map/conv_general_dilated | solution.py:26
  82.2 0.0 copy-start.7
  82.2 0.1 copy.49
  82.3 0.0 copy-done.5
  82.3 0.0 copy-done.9
  82.3 0.0 copy-done.10
  82.3 2.8 %add_convert_fusion.1.y_ref = bf16[6,128,1152]{2,1,0:T(8,128)(2,1)S(1)} fusion(f32[6,4,32,1152]{3,2,1,0:T(8,128)} %copy.38, f32[1152]{0:T(1024)S(1)} %copy-done.9, f32[1152]{0:T(1024)S(1)} %copy-done.10, f32[6,128]{1,0:T(8,128)S(1)} %copy.48, f32[6,128]{1,0:T(8,128)S(1)} %copy.49, f32[128,1152]{1,0:T(8,128)S(1)} %copy-done.5, f32[1152]{0:T(1024)S(1)} %copy-done.6), kind=kLoop, calls=%fused_computation.11 | loop fusion | flops 7962624 | bytes 5918208 | tf_op jit(solution)/shard_map/convert_element_type | solution.py:341
  85.1 0.0 copy-done.7
  85.1 1.7 reshape.65.bias_ref
  86.9 0.0 copy-start.3
  86.9 64.0 %attend.1 = bf16[6,16,72,128]{3,2,1,0:T(8,128)(2,1)S(1)} custom-call(bf16[6,128,1152]{2,1,0:T(8,128)(2,1)S(1)} %add_convert_fusion.1.y_ref, f32[3456,1]{1,0:T(8,128)} %reshape.65.bias_ref, bf16[3456,1152]{1,0:T(8,128)(2,1)} %bitcast.30), custom_call_target="tpu_custom_call" | custom-call | tf_op jit(solution)/shard_map/attend/pallas_call | solution.py:235
  150.9 0.0 copy-start.2
  150.9 1.2 copy-done.2
  152.1 0.0 copy-start.8
  152.1 0.0 copy-start.11
  152.1 0.0 copy-start.12
  152.1 0.0 copy-start.13
  152.1 0.0 copy-start.14
  152.1 0.0 copy-done.3
  152.1 1.6 fusion.2.x_ref
  153.7 0.0 copy-done.8
  153.7 0.6 broadcast_in_dim.24.b1_ref
  154.3 0.0 copy-done.11
  154.3 0.6 broadcast_in_dim.10.bo_ref
  154.9 0.0 copy-done.12
  154.9 0.6 broadcast_in_dim.22.g2_ref
  155.5 0.0 copy-done.13
  155.5 0.6 broadcast_in_dim.23.c2_ref
  156.1 0.0 copy-done.14
  156.1 0.6 broadcast_in_dim.25.b2_ref
  156.7 0.0 copy-start.1
  156.7 31.6 %mlp.1 = bf16[768,1152]{1,0:T(8,128)(2,1)} custom-call(bf16[6,1152,128]{2,1,0:T(8,128)(2,1)} %bitcast.27, bf16[768,1152]{1,0:T(8,128)(2,1)} %fusion.2.x_ref, bf16[1152,1152]{1,0:T(8,128)(2,1)} %bitcast.34, f32[1,1152]{1,0:T(1,128)} %broadcast_in_dim.10.bo_ref, f32[1,1152]{1,0:T(1,128)} %broadcast_in_dim.22.g2_ref, f32[1,1152]{1,0:T(1,128)} %broadcast_in_dim.23.c2_ref, ...), custom_call_target="tpu_custom_call" | custom-call | flops 17270046720 | bytes 33554432 | tf_op jit(solution)/shard_map/mlp/pallas_call | solution.py:319
  188.4 0.0 copy-done.1
  (2 shorter events, 0.0 us)
Async XLA Ops:
  0.0 24.2 %copy-start = (bf16[14,14,3,1152]{3,1,2,0:T(8,128)(2,1)S(1)}, bf16[14,14,3,1152]{3,1,2,0:T(8,128)(2,1)}, u32[]{:S(2)}) copy-start(bf16[14,14,3,1152]{3,1,2,0:T(8,128)(2,1)} %param.17) | copy-start | bytes 4064260
  1.1 72.7 %copy-start.4 = (f32[128,1152]{1,0:T(8,128)}, f32[128,1152]{1,0:T(8,128)S(1)}, u32[]{:S(2)}) copy-start(f32[128,1152]{1,0:T(8,128)S(1)} %convert_element_type.27) | copy-start | bytes 1769476
  3.1 21.1 %copy-start.6 = (f32[1152]{0:T(1024)S(1)}, f32[1152]{0:T(1024)}, u32[]{:S(2)}) copy-start(f32[1152]{0:T(1024)} %param.18) | copy-start | bytes 13828
  77.3 4.9 %copy-start.5 = (f32[128,1152]{1,0:T(8,128)S(1)}, f32[128,1152]{1,0:T(8,128)}, u32[]{:S(2)}) copy-start(f32[128,1152]{1,0:T(8,128)} %copy-done.4) | copy-start | bytes 1769476
  77.3 4.9 %copy-start.9 = (f32[1152]{0:T(1024)S(1)}, f32[1152]{0:T(1024)}, u32[]{:S(2)}) copy-start(f32[1152]{0:T(1024)} %param.21) | copy-start | bytes 13828
  77.3 4.9 %copy-start.10 = (f32[1152]{0:T(1024)S(1)}, f32[1152]{0:T(1024)}, u32[]{:S(2)}) copy-start(f32[1152]{0:T(1024)} %param.20) | copy-start | bytes 13828
  82.2 2.9 %copy-start.7 = (f32[3,16,72]{2,1,0:T(8,128)S(1)}, f32[3,16,72]{2,1,0:T(8,128)}, u32[]{:S(2)}) copy-start(f32[3,16,72]{2,1,0:T(8,128)} %param.23) | copy-start | bytes 41476
  86.9 65.3 %copy-start.3 = (f32[6,4,32,1152]{3,2,1,0:T(8,128)S(1)}, f32[6,4,32,1152]{3,2,1,0:T(8,128)}, u32[]{:S(2)}) copy-start(f32[6,4,32,1152]{3,2,1,0:T(8,128)} %copy.38) | copy-start | bytes 10616836
  150.9 1.2 copy-start.2
  152.1 1.6 copy-start.8
  152.1 2.2 %copy-start.11 = (f32[1152]{0:T(1024)S(1)}, f32[1152]{0:T(1024)}, u32[]{:S(2)}) copy-start(f32[1152]{0:T(1024)} %param.25) | copy-start | bytes 13828
  152.1 2.8 %copy-start.12 = (f32[1152]{0:T(1024)S(1)}, f32[1152]{0:T(1024)}, u32[]{:S(2)}) copy-start(f32[1152]{0:T(1024)} %param.26) | copy-start | bytes 13828
  152.1 3.4 %copy-start.13 = (f32[1152]{0:T(1024)S(1)}, f32[1152]{0:T(1024)}, u32[]{:S(2)}) copy-start(f32[1152]{0:T(1024)} %param.27) | copy-start | bytes 13828
  152.1 4.0 %copy-start.14 = (f32[1152]{0:T(1024)S(1)}, f32[1152]{0:T(1024)}, u32[]{:S(2)}) copy-start(f32[1152]{0:T(1024)} %param.31) | copy-start | bytes 13828
  156.7 31.6 %copy-start.1 = (bf16[14,14,3,1152]{3,1,2,0:T(8,128)(2,1)S(1)}, bf16[14,14,3,1152]{3,1,2,0:T(8,128)(2,1)}, u32[]{:S(2)}) copy-start(bf16[14,14,3,1152]{3,1,2,0:T(8,128)(2,1)} %param.17) | copy-start | bytes 4064260

commit v2 on v1

--- a/solution.py
+++ b/solution.py
@@ -2,6 +2,7 @@
 import math
 import jax
 import jax.numpy as jnp
+import numpy as np
 from jax import lax
 from jax.experimental import pallas as pl
 from jax.experimental.pallas import tpu as pltpu
@@ -20,14 +21,91 @@
     return centered * lax.rsqrt(variance + LN_EPS) * ln_gain + ln_bias
 
 
-def embed_tokens(images, w_patch, b_patch, pos_embed):
-    num_images, num_rows, num_cols, channels = images.shape
-    patch_len = w_patch.shape[0]
-    patch_embed = lax.conv_general_dilated(
-        images.astype(BF16), w_patch, (patch_len, patch_len), 'VALID',
-        dimension_numbers=('NHWC', 'HWIO', 'NHWC'), preferred_element_type=F32)
-    patch_embed = patch_embed.reshape(num_images, -1, w_patch.shape[3])
-    return (patch_embed + b_patch + pos_embed.astype(F32)).astype(BF16)
+def embed_kernel(patch, img_ref, w_ref, sel_ref, pos_ref, bp_ref, g1_ref, c1_ref, x_out, y_out,
+                 w_f, w_s, rows_s, perm_s, x_t):
+    n_img, chan, height, width = img_ref.shape
+    cols = width // patch
+    grid_rows = height // patch
+    slab = sel_ref.shape[0] // grid_rows
+    band = grid_rows * cols
+    lanes = 128
+    per_tile = lanes // cols
+
+    def weights(n, carry):
+        tile = pl.ds(pl.multiple_of(n * lanes, lanes), lanes)
+        for q in range(patch):
+            w_f[n, q * slab + slab - 8:(q + 1) * slab] = jnp.zeros((8, lanes), F32)
+        for p in range(patch):
+            for c in range(chan):
+                w_f[n, pl.ds(c * patch + p, patch, stride=slab), :] = w_ref[p, c, :, tile].astype(F32)
+        w_s[:, tile] = w_f[n].astype(BF16)
+        return carry
+
+    lax.fori_loop(0, w_f.shape[0], weights, 0)
+
+    out_col = lax.broadcasted_iota(jnp.int32, (1, width), 1)
+    source = lax.rem(out_col, cols) * patch + out_col // cols
+    perm_s[...] = jnp.where(lax.broadcasted_iota(jnp.int32, (width, width), 0) == source, 1.0, 0.0).astype(BF16)
+    for i in range(n_img):
+        pixels = img_ref[i].reshape(chan * height, width).astype(BF16)
+        rows_s[i] = jnp.dot(sel_ref[...], pixels, preferred_element_type=F32).astype(BF16)
+
+    lane_group = lax.broadcasted_iota(jnp.int32, (slab, lanes), 1) // cols
+
+    def patches(i, carry):
+        z = jnp.dot(rows_s[i], perm_s[...], preferred_element_type=F32)
+        z = jnp.concatenate([z, jnp.zeros((z.shape[0], -width % lanes), F32)], axis=1)
+        for q in range(patch):
+            tile, off = q // per_tile, q % per_tile
+            block = jnp.zeros((slab, lanes), F32)
+            for y in range(grid_rows):
+                part = z[y * slab:(y + 1) * slab, tile * lanes:(tile + 1) * lanes]
+                shift = (y - off) % per_tile * cols
+                if shift:
+                    part = pltpu.roll(part, shift, 1)
+                block = jnp.where(lane_group == y, part, block)
+            x_t[i, q * slab:(q + 1) * slab] = block.astype(BF16)
+        return carry
+
+    lax.fori_loop(0, n_img, patches, 0)
+
+    def embed(i, carry):
+        x0 = lax.dot_general(x_t[i], w_s[...], (((0,), (0,)), ((), ())), preferred_element_type=F32)
+        x0 = (x0 + bp_ref[...] + pos_ref[...].astype(F32)).astype(BF16)
+        x_out[i] = x0
+        y_out[i] = layer_norm(x0.astype(F32), g1_ref[...], c1_ref[...]).astype(BF16)
+        return carry
+
+    lax.fori_loop(0, n_img, embed, 0)
+
+
+def embed_tokens(images, w_patch, b_patch, pos_embed, ln1_gain, ln1_bias):
+    n_img, height, width, chan = images.shape
+    patch, dim = w_patch.shape[0], w_patch.shape[3]
+    grid_rows = height // patch
+    band = pos_embed.shape[0]
+    slab = -(-chan * patch // 16) * 16
+    select = np.zeros((grid_rows * slab, chan * height), np.float32)
+    for y in range(grid_rows):
+        for c in range(chan):
+            for p in range(patch):
+                select[y * slab + c * patch + p, c * height + y * patch + p] = 1.0
+    vmem = pl.BlockSpec(memory_space=pltpu.VMEM)
+    depth = patch * slab
+    return pl.pallas_call(
+        functools.partial(embed_kernel, patch),
+        out_shape=[jax.ShapeDtypeStruct((n_img, band, dim), BF16)] * 2,
+        in_specs=[vmem] * 7,
+        out_specs=[vmem] * 2,
+        scratch_shapes=[
+            pltpu.VMEM((dim // 128, depth, 128), F32), pltpu.VMEM((depth, dim), BF16),
+            pltpu.VMEM((n_img, grid_rows * slab, width), BF16), pltpu.VMEM((width, width), BF16),
+            pltpu.VMEM((n_img, depth, band), BF16),
+        ],
+        compiler_params=pltpu.CompilerParams(vmem_limit_bytes=32 * 2**20),
+        name='embed',
+    )(jnp.transpose(images, (0, 3, 1, 2)), jnp.transpose(w_patch, (0, 2, 1, 3)), jnp.asarray(select, BF16), pos_embed,
+      b_patch[None], ln1_gain[None], ln1_bias[None])
 
 
 def attend_kernel(n_chip, scale, y_ref, bias_ref, w_hbm, o_out,
@@ -104,9 +182,9 @@
             for g in range(0, heads, step):
                 prod = lax.dot_general(w_u[t, g * 72:(g + step) * 72], y_chunk, (((1,), (1,)), ((), ())),
                                        preferred_element_type=F32)
+                bias = bias_ref[t, pl.ds(h0 + g, step)].T
                 for h in range(step):
-                    row0 = pl.multiple_of(t * dim + (h0 + g + h) * 72, 8)
-                    val = prod[h * 72:(h + 1) * 72] + bias_ref[pl.ds(row0, 72)]
+                    val = prod[h * 72:(h + 1) * 72] + bias[:, h:h + 1]
                     if t == 1:
                         qkv[t][g + h, 256 * j:256 * (j + 1), :] = val.T.astype(BF16)
                     else:
@@ -218,7 +296,7 @@
                     device_id={'sp': sib}, device_id_type=MESH).wait_recv()
 
 
-def attend_layer(normed, w_qkv_t, bias_col, n_dev, num_heads, head_dim):
+def attend_layer(normed, w_qkv_t, b_qkv, n_dev, num_heads, head_dim):
     images, band, dim = normed.shape
     n_chip = n_dev // 2
     heads_b, heads_a = num_heads // 4, num_heads // 2
@@ -249,7 +327,7 @@
         ],
         compiler_params=pltpu.CompilerParams(collective_id=0, has_side_effects=True, vmem_limit_bytes=50 * 2**20),
         name='attend',
-    )(normed, bias_col, w_qkv_t)
+    )(normed, b_qkv, w_qkv_t)
 
 
 def mlp_kernel(chunk, tail, o_ref, x_ref, wo_ref, bo_ref, g2_ref, c2_ref, b1_ref, b2_ref, w1_hbm, w2_hbm, out_ref,
@@ -337,10 +415,9 @@
 
     def device_step(images, w_patch, b_patch, pos_embed, ln1_gain, ln1_bias, w_qkv, b_qkv, w_out, b_out, ln2_gain, ln2_bias, w_fc1, b_fc1, w_fc2, b_fc2):
         dim, _, num_heads, head_dim = w_qkv.shape
-        x_zero = embed_tokens(images, w_patch, b_patch, pos_embed)
-        normed = layer_norm(x_zero.astype(F32), ln1_gain, ln1_bias).astype(BF16)
+        x_zero, normed = embed_tokens(images, w_patch, b_patch, pos_embed, ln1_gain, ln1_bias)
         w_qkv_t = jnp.transpose(w_qkv, (1, 2, 3, 0)).reshape(3 * dim, dim)
-        o_t = attend_layer(normed, w_qkv_t, b_qkv.reshape(3 * dim, 1), n_dev, num_heads, head_dim)
+        o_t = attend_layer(normed, w_qkv_t, b_qkv, n_dev, num_heads, head_dim)
         num_images, band = normed.shape[:2]
         out = mlp_layer(o_t.reshape(num_images, dim, band), x_zero.reshape(num_images * band, dim), w_out.reshape(dim, dim),
                         b_out, ln2_gain, ln2_bias, w_fc1.T, b_fc1, w_fc2, b_fc2)

time: 189 us -> 119 us (0.63)
  matrix products: 49.6 us -> 0 us
  local copies, waits for them, and re-layouts: 32.1 us -> 15.9 us
  other arithmetic: 10.9 us -> 0 us
  Pallas kernels: 95.6 us -> 103 us
    conv_general_dilated x1 -> x0, matrix products: 49.6 us -> none  [embed_tokens(): lax.conv_general_dilated(images.astype(BF16), w_patch, (patch_len, patch_...]
    convert_element_type x1 -> x0, local copies, waits for them, and re-layouts: 21.1 us -> none  [embed_tokens(): images.astype(BF16)]
    pallas_call x0 -> x1, Pallas kernels: none -> 8.55 us  [embed_tokens(): pl.pallas_call(functools.partial(embed_kernel, patch), out_shape=[jax.Sha...]
    convert_element_type x4 -> x0, other arithmetic: 7.47 us -> none  [the longest x1 2.83 us: device_step(): normed = layer_norm(x_zero.astype(F32), ln1_gain, ln1_bias).astype(BF16)]
    unnamed x30 -> x14, local copies, waits for them, and re-layouts: 1.29 us -> 7.27 us
    conv_general_dilated x1 -> x0, local copies, waits for them, and re-layouts: 4.85 us -> none  [embed_tokens(): lax.conv_general_dilated(images.astype(BF16), w_patch, (patch_len, patch_...]
    reduce_sum x1 -> x0, other arithmetic: 3.44 us -> none  [layer_norm(): variance = jnp.mean(centered * centered, axis=-1, keepdims=True)]
    broadcast_in_dim x0 -> x3, local copies, waits for them, and re-layouts: none -> 2.11 us  [the longest x1 0.71 us: embed_tokens(): ln1_bias[None]]
where the time goes in v2:
time: 119 us
  Pallas kernels  103 us (87%)
  local copies, waits for them, and re-layouts  15.9 us (13%)
    pallas_call x1, Pallas kernels, attend_layer(): pl.pallas_call(functools.partial(attend_kernel, n_chip, scale), out_shape...  62.5 us
    pallas_call x1, Pallas kernels, mlp_layer(): pl.pallas_call(functools.partial(mlp_kernel, chunk, tail), out_shape=jax....  31.7 us
    pallas_call x1, Pallas kernels, embed_tokens(): pl.pallas_call(functools.partial(embed_kernel, patch), out_shape=[jax.Sha...  8.55 us
    unnamed x14, local copies, waits for them, and re-layouts  7.27 us

profile of v2, /device:TPU:113, one launch (start us, length us, event | category | flops | bytes accessed | tf_op | source)
XLA Modules:
  0.0 118.8 jit_solution(5875346607535986534)
XLA Ops:
  0.0 0.7 broadcast_in_dim.24.bp_ref
  0.7 0.7 broadcast_in_dim.25.g1_ref
  1.4 0.0 copy-start.5
  1.4 0.7 broadcast_in_dim.26.c1_ref
  2.1 1.3 %broadcast_in_dim.27.bo_ref = f32[1,1152]{1,0:T(1,128)} reshape(f32[1152]{0:T(1024)} %param.26) | data formatting | bytes 9216 | tf_op jit(solution)/shard_map/broadcast_in_dim | solution.py:410
  3.4 1.3 %broadcast_in_dim.28.g2_ref = f32[1,1152]{1,0:T(1,128)} reshape(f32[1152]{0:T(1024)} %param.27) | data formatting | bytes 9216 | tf_op jit(solution)/shard_map/broadcast_in_dim | solution.py:410
  4.7 1.3 %broadcast_in_dim.29.c2_ref = f32[1,1152]{1,0:T(1,128)} reshape(f32[1152]{0:T(1024)} %param.28) | data formatting | bytes 9216 | tf_op jit(solution)/shard_map/broadcast_in_dim | solution.py:410
  6.0 1.3 %broadcast_in_dim.31.b2_ref = f32[1,1152]{1,0:T(1,128)} reshape(f32[1152]{0:T(1024)} %param.32) | data formatting | bytes 9216 | tf_op jit(solution)/shard_map/broadcast_in_dim | solution.py:410
  7.3 1.3 %broadcast_in_dim.30.b1_ref = f32[1,4304]{1,0:T(1,128)} reshape(f32[4304]{0:T(1024)} %param.30) | data formatting | bytes 34432 | tf_op jit(solution)/shard_map/broadcast_in_dim | solution.py:410
  8.6 0.0 copy-start
  8.6 1.6 %copy-done = f32[6,56,448,3]{2,1,3,0:T(8,128)S(1)} copy-done((f32[6,56,448,3]{2,1,3,0:T(8,128)S(1)}, f32[6,56,448,3]{2,1,3,0:T(8,128)}, u32[]{:S(2)}) %copy-start) | copy-done | bytes 1806360
  10.2 0.0 copy-start.2
  10.2 1.4 %copy-done.2 = bf16[14,14,3,1152]{3,1,2,0:T(8,128)(2,1)S(1)} copy-done((bf16[14,14,3,1152]{3,1,2,0:T(8,128)(2,1)S(1)}, bf16[14,14,3,1152]{3,1,2,0:T(8,128)(2,1)}, u32[]{:S(2)}) %copy-start.2) | copy-done | bytes 1354776
  11.6 0.0 copy-start.3
  11.6 1.0 copy-done.3
  12.6 0.0 copy-start.4
  12.6 0.9 copy-done.4
  13.4 8.5 %embed.1 = (bf16[6,128,1152]{2,1,0:T(8,128)(2,1)S(1)}, bf16[6,128,1152]{2,1,0:T(8,128)(2,1)S(1)}) custom-call(f32[6,3,56,448]{3,2,1,0:T(8,128)S(1)} %bitcast.10, bf16[14,3,14,1152]{3,2,1,0:T(8,128)(2,1)S(1)} %bitcast.12, bf16[192,168]{1,0:T(8,128)(2,1)S(1)} %copy-done.4, bf16[128,1152]{1,0:T(8,128)(2,1)S(1)} %copy-done.3, ...), custom_call_target="tpu_custom_call" | custom-call | tf_op jit(solution)/shard_map/embed/pallas_call | solution.py:95
  22.0 0.0 copy-start.6
  22.0 1.2 %copy-done.6 = bf16[6,128,1152]{2,1,0:T(8,128)(2,1)} copy-done((bf16[6,128,1152]{2,1,0:T(8,128)(2,1)}, bf16[6,128,1152]{2,1,0:T(8,128)(2,1)S(1)}, u32[]{:S(2)}) %copy-start.6) | copy-done | bytes 1769496
  23.2 0.0 copy-done.5
  23.2 62.5 %attend.1 = bf16[6,16,72,128]{3,2,1,0:T(8,128)(2,1)S(1)} custom-call(bf16[6,128,1152]{2,1,0:T(8,128)(2,1)S(1)} %get-tuple-element.7.y_ref, f32[3,16,72]{2,1,0:T(8,128)S(1)} %copy-done.5, bf16[3456,1152]{1,0:T(8,128)(2,1)} %bitcast.14), custom_call_target="tpu_custom_call" | custom-call | tf_op jit(solution)/shard_map/attend/pallas_call | solution.py:313
  85.8 0.0 copy-start.1
  85.8 1.2 %copy-done.1 = bf16[6,16,72,128]{3,2,1,0:T(8,128)(2,1)} copy-done((bf16[6,16,72,128]{3,2,1,0:T(8,128)(2,1)}, bf16[6,16,72,128]{3,2,1,0:T(8,128)(2,1)S(1)}, u32[]{:S(2)}) %copy-start.1) | copy-done | bytes 1769496
  87.0 31.7 %mlp.1 = bf16[768,1152]{1,0:T(8,128)(2,1)} custom-call(bf16[6,1152,128]{2,1,0:T(8,128)(2,1)} %bitcast.11, bf16[768,1152]{1,0:T(8,128)(2,1)} %bitcast.13, bf16[1152,1152]{1,0:T(8,128)(2,1)} %bitcast.16, f32[1,1152]{1,0:T(1,128)} %broadcast_in_dim.27.bo_ref, f32[1,1152]{1,0:T(1,128)} %broadcast_in_dim.28.g2_ref, f32[1,1152]{1,0:T(1,128)} %broadcast_in_dim.29.c2_ref, ...), custom_call_target="tpu_custom_call" | custom-call | flops 17270046720 | bytes 33554432 | tf_op jit(solution)/shard_map/mlp/pallas_call | solution.py:397
Async XLA Ops:
  1.4 21.8 %copy-start.5 = (f32[3,16,72]{2,1,0:T(8,128)S(1)}, f32[3,16,72]{2,1,0:T(8,128)}, u32[]{:S(2)}) copy-start(f32[3,16,72]{2,1,0:T(8,128)} %bias_ref.1) | copy-start | bytes 41476
  8.6 1.6 %copy-start = (f32[6,56,448,3]{2,1,3,0:T(8,128)S(1)}, f32[6,56,448,3]{2,1,3,0:T(8,128)}, u32[]{:S(2)}) copy-start(f32[6,56,448,3]{2,1,3,0:T(8,128)} %param.17) | copy-start | bytes 5419012
  10.2 1.4 %copy-start.2 = (bf16[14,14,3,1152]{3,1,2,0:T(8,128)(2,1)S(1)}, bf16[14,14,3,1152]{3,1,2,0:T(8,128)(2,1)}, u32[]{:S(2)}) copy-start(bf16[14,14,3,1152]{3,1,2,0:T(8,128)(2,1)} %param.18) | copy-start | bytes 4064260
  11.6 1.0 copy-start.3
  12.6 0.9 copy-start.4
  22.0 1.2 %copy-start.6 = (bf16[6,128,1152]{2,1,0:T(8,128)(2,1)}, bf16[6,128,1152]{2,1,0:T(8,128)(2,1)S(1)}, u32[]{:S(2)}) copy-start(bf16[6,128,1152]{2,1,0:T(8,128)(2,1)S(1)} %get-tuple-element.8) | copy-start | bytes 5308420
  85.8 1.2 %copy-start.1 = (bf16[6,16,72,128]{3,2,1,0:T(8,128)(2,1)}, bf16[6,16,72,128]{3,2,1,0:T(8,128)(2,1)S(1)}, u32[]{:S(2)}) copy-start(bf16[6,16,72,128]{3,2,1,0:T(8,128)(2,1)S(1)} %attend.1) | copy-start | bytes 5308420

commit v3 on v0

v3 whole, which is shorter than its diff:
```python
import functools
import math
import jax
import jax.numpy as jnp
import numpy as np
from jax import lax
from jax.experimental import pallas as pl
from jax.experimental.pallas import tpu as pltpu
from jax.sharding import PartitionSpec as P

LN_EPS = 1e-6
MESH = pl.DeviceIdType.MESH
F32 = jnp.float32
BF16 = jnp.bfloat16


def layer_norm(x_in, ln_gain, ln_bias):
    row_mean = jnp.mean(x_in, axis=-1, keepdims=True)
    centered = x_in - row_mean
    variance = jnp.mean(centered * centered, axis=-1, keepdims=True)
    return centered * lax.rsqrt(variance + LN_EPS) * ln_gain + ln_bias


def front_kernel(dims, img_hbm, wp_hbm, wq_hbm, pos_hbm, sel_ref, bp_ref, g1_ref, c1_ref, bq_ref, x_out, o_out,
                 img, wp, pos, w_f, w_s, perm_s, y_own, y_b, y_a, w_b, w_a, q_b, k_b, v_b, q_a, k_a, v_a,
                 s_buf, m_buf, p_buf, l_buf, o_b, o_a,
                 i_sem, p_sem, w_sem, y_send, y_recv, f_send, f_recv, o_send, o_recv):
    patch, n_dev, scale = dims
    n_chip = n_dev // 2
    n_img, chan, height, width = img.shape
    dim = y_own.shape[2]
    hd = v_a.shape[1]
    me = lax.axis_index('sp')
    chip = me // 2
    core = lax.rem(me, 2)
    sib = chip * 2 + (1 - core)
    heads = (w_b.shape[1] // hd, w_a.shape[1] // hd)
    head0 = ((lax.rem(chip, 2) * 2 + core) * heads[0], core * heads[1])
    y_units, w_units, o_units = (y_b, y_a), (w_b, w_a), (o_b, o_a)
    qkv_units = ((q_b, k_b, v_b), (q_a, k_a, v_a))

    def offset(b):
        return 2 - b + 3 * (b // 2) - 2 * (b // 3)

    def back(b):
        return (2 * b) % 3 + 3 * (b // 3)

    def owner_of(b):
        return lax.rem(chip + offset(b), n_chip)

    def image_of(owner, u):
        return (owner // 2) * 3 + (1 if u == 0 else 2 * lax.rem(owner, 2))

    order = [(1, 0), (1, 1), (1, 2), (1, 3), (0, 0), (0, 3)]
    wp_copy = pltpu.make_async_copy(wp_hbm, wp, p_sem.at[0])
    pos_copy = pltpu.make_async_copy(pos_hbm, pos, p_sem.at[1])
    wp_copy.start()
    img_copies = []
    for n, (u, b) in enumerate(order):
        c = pltpu.make_async_copy(img_hbm.at[image_of(owner_of(b), u)], img.at[n], i_sem.at[n])
        c.start()
        img_copies.append(c)
        if n == 0:
            pos_copy.start()
    w_copies = {}
    for u in (1, 0):
        for t in range(3):
            rows = heads[u] * hd
            c = pltpu.make_async_copy(
                wq_hbm.at[pl.ds(pl.multiple_of(t * dim + head0[u] * hd, 8), rows)], w_units[u].at[t], w_sem.at[u, t])
            c.start()
            w_copies[u, t] = c

    barrier = pltpu.get_barrier_semaphore()
    for j in range(1, n_dev):
        pl.semaphore_signal(barrier, inc=1, device_id={'sp': lax.rem(me + j, n_dev)}, device_id_type=MESH)

    cols = width // patch
    grid_rows = height // patch
    slab = sel_ref.shape[0] // grid_rows
    lanes = 128
    per_tile = lanes // cols
    out_col = lax.broadcasted_iota(jnp.int32, (1, width), 1)
    source = lax.rem(out_col, cols) * patch + out_col // cols
    perm_s[...] = jnp.where(lax.broadcasted_iota(jnp.int32, (width, width), 0) == source, 1.0, 0.0).astype(BF16)
    wp_copy.wait()

    def weights(n, carry):
        tile = pl.ds(pl.multiple_of(n * lanes, lanes), lanes)
        for q in range(patch):
            w_f[n, q * slab + slab - 8:(q + 1) * slab] = jnp.zeros((8, lanes), F32)
        for p in range(patch):
            for c in range(chan):
                w_f[n, pl.ds(c * patch + p, patch, stride=slab), :] = wp[p, c, :, tile].astype(F32)
        w_s[:, tile] = w_f[n].astype(BF16)
        return carry

    lax.fori_loop(0, w_f.shape[0], weights, 0)
    pos_copy.wait()
    lane_group = lax.broadcasted_iota(jnp.int32, (slab, lanes), 1) // cols

    def embed(n):
        u, b = order[n]
        img_copies[n].wait()
        pixels = img[n].reshape(chan * height, width).astype(BF16)
        rows = jnp.dot(sel_ref[...], pixels, preferred_element_type=F32).astype(BF16)
        z = jnp.dot(rows, perm_s[...], preferred_element_type=F32)
        z = jnp.concatenate([z, jnp.zeros((z.shape[0], -width % lanes), F32)], axis=1)
        blocks = []
        for q in range(patch):
            tile, off = q // per_tile, q % per_tile
            block = jnp.zeros((slab, lanes), F32)
            for y in range(grid_rows):
                part = z[y * slab:(y + 1) * slab, tile * lanes:(tile + 1) * lanes]
                shift = (y - off) % per_tile * cols
                if shift:
                    part = pltpu.roll(part, shift, 1)
                block = jnp.where(lane_group == y, part, block)
            blocks.append(block.astype(BF16))
        x_t = jnp.concatenate(blocks, axis=0)
        x0 = lax.dot_general(x_t, w_s[...], (((0,), (0,)), ((), ())), preferred_element_type=F32)
        x0 = (x0 + bp_ref[...].reshape(1, dim) + pos[...].astype(F32)).astype(BF16)
        i = image_of(owner_of(b), u)
        x_out[i] = x0
        y_own[i] = layer_norm(x0.astype(F32), g1_ref[...].reshape(1, dim), c1_ref[...].reshape(1, dim)).astype(BF16)

    def y_copy(u, b):
        return pltpu.make_async_remote_copy(
            y_own.at[image_of(owner_of(b), u)], y_units[u].at[back(b), core], y_send.at[u, b], y_recv.at[u, back(b)],
            device_id={'sp': owner_of(b) * 2 + core}, device_id_type=MESH)

    def own_copy(u):
        return pltpu.make_async_remote_copy(
            y_own.at[image_of(chip, u)], y_units[u].at[3, core], f_send.at[u, 3], f_recv.at[u, 3],
            device_id={'sp': sib}, device_id_type=MESH)

    def forward(u, b):
        return pltpu.make_async_remote_copy(
            y_units[u].at[b, core], y_units[u].at[b, core], f_send.at[u, b], f_recv.at[u, b],
            device_id={'sp': sib}, device_id_type=MESH)

    def send_y(n):
        u, b = order[n]
        if n < 3:
            y_copy(u, b).start()
        elif n == 3:
            own_copy(1).start()
        elif n == 4:
            y_copy(0, 0).start()
        else:
            y_copy(0, 1).start()
            y_copy(0, 2).start()
            own_copy(0).start()
        if b == 3:
            y_units[u][3, core] = y_own[image_of(chip, u)]

    embed(0)
    pl.semaphore_wait(barrier, n_dev - 1)
    for n in range(1, n_img):
        embed(n)
        send_y(n - 1)

    def project(u, b):
        y_chunk = y_units[u][b].reshape(-1, dim)
        width_b = y_chunk.shape[0]
        step = 4
        for t in range(3):
            for g in range(0, heads[u], step):
                prod = lax.dot_general(w_units[u][t, g * hd:(g + step) * hd], y_chunk, (((1,), (1,)), ((), ())),
                                       preferred_element_type=F32)
                bias = bq_ref[t, pl.ds(head0[u] + g, step)].T
                for h in range(step):
                    val = prod[h * hd:(h + 1) * hd] + bias[:, h:h + 1]
                    if t == 1:
                        qkv_units[u][t][g + h, width_b * b:width_b * (b + 1), :] = val.T.astype(BF16)
                    else:
                        qkv_units[u][t][g + h, :, width_b * b:width_b * (b + 1)] = val.astype(BF16)

    blk_len = s_buf.shape[2]

    def attend(u):
        q_u, k_u, v_u = qkv_units[u]
        o_u = o_units[u]
        n_head = heads[u]
        n_item = n_head * n_chip

        def scores(item, slot):
            h = lax.rem(item, n_head)
            blk = pl.ds(pl.multiple_of(item // n_head * blk_len, blk_len), blk_len)
            sc = jnp.dot(k_u[h], q_u[h, :, blk], preferred_element_type=F32)
            s_buf[slot] = sc
            m_buf[slot] = jnp.broadcast_to(jnp.max(sc, axis=0, keepdims=True), (8, blk_len))

        def weigh(slot):
            e = jnp.exp2((s_buf[slot] - m_buf[slot, :1]) * scale)
            l_buf[slot] = jnp.broadcast_to(jnp.sum(e, axis=0, keepdims=True), (8, blk_len))
            p_buf[slot] = e.astype(BF16)

        def mix(item, slot):
            h = lax.rem(item, n_head)
            b = item // n_head
            o = jnp.dot(v_u[h], p_buf[slot], preferred_element_type=F32) * (1.0 / l_buf[slot, :1])
            o = o.astype(BF16)
            o_u[b, 0, h] = o[:, :blk_len // 2]
            o_u[b, 1, h] = o[:, blk_len // 2:]

        scores(jnp.int32(0), 0)
        weigh(0)
        scores(jnp.int32(1), 1)

        def body(i, carry):
            scores(2 * i + 2, 0)
            weigh(1)
            mix(2 * i, 0)
            scores(2 * i + 3, 1)
            weigh(0)
            mix(2 * i + 1, 1)

            @pl.when((lax.rem(2 * i, n_head) == 0) & (i > 0))
            def _():
                send_o(u, (2 * i) // n_head - 1)
            return carry

        lax.fori_loop(0, n_item // 2 - 1, body, 0)
        weigh(1)
        mix(jnp.int32(n_item - 2), 0)
        mix(jnp.int32(n_item - 1), 1)

    def o_dst(owner, u, own_core):
        first = (lax.rem(owner, 2) * 2 + own_core) * heads[0] if u == 0 else own_core * heads[1]
        return o_out.at[image_of(owner, u), pl.ds(first, heads[u])]

    def o_copy(u, b, c2):
        dst_core = core if c2 == 0 else 1 - core
        return pltpu.make_async_remote_copy(
            o_units[u].at[b, dst_core], o_dst(chip, u, core), o_send.at[u, b, c2], o_recv.at[u, back(b), c2],
            device_id={'sp': owner_of(b) * 2 + dst_core}, device_id_type=MESH)

    def o_local(u):
        return pltpu.make_async_copy(o_units[u].at[3, core], o_dst(chip, u, core), o_recv.at[u, 3, 0])

    def send_o(u, b):
        if isinstance(b, int) and b == 3:
            o_copy(u, 3, 1).start()
            o_local(u).start()
        else:
            o_copy(u, b, 0).start()
            o_copy(u, b, 1).start()

    def gather(u, b):
        if b < 3:
            y_copy(u, back(b)).wait_recv()
            forward(u, b).start()
            pltpu.make_async_remote_copy(
                y_units[u].at[b, 1 - core], y_units[u].at[b, 1 - core], f_send.at[u, b], f_recv.at[u, b],
                device_id={'sp': sib}, device_id_type=MESH).wait_recv()
        else:
            own_copy(u).wait_recv()

    for t in range(3):
        w_copies[1, t].wait()
    gather(1, 3)
    project(1, 3)
    send_y(n_img - 1)
    for t in range(3):
        w_copies[0, t].wait()
    gather(0, 3)
    project(0, 3)
    for b in (1, 2, 0):
        gather(1, b)
        project(1, b)
    attend(1)
    send_o(1, 3)
    for b in (1, 2, 0):
        gather(0, b)
        project(0, b)
    attend(0)
    send_o(0, 3)

    for u in range(2):
        own_copy(u).wait_send()
        for b in range(3):
            y_copy(u, b).wait_send()
            forward(u, b).wait_send()
            for c2 in range(2):
                o_copy(u, b, c2).wait_send()
        o_copy(u, 3, 1).wait_send()
        o_local(u).wait()
    for u in range(2):
        for b in range(n_chip):
            for c2 in range(2):
                if b == 3 and c2 == 0:
                    continue
                src_core = core if c2 == 0 else 1 - core
                pltpu.make_async_remote_copy(
                    o_units[u].at[b, 0], o_dst(owner_of(b), u, src_core), o_send.at[u, b, c2], o_recv.at[u, b, c2],
                    device_id={'sp': sib}, device_id_type=MESH).wait_recv()


def front_layer(images, w_patch, b_patch, pos_embed, ln1_gain, ln1_bias, w_qkv, b_qkv, n_dev):
    n_img, height, width, chan = images.shape
    patch, dim = w_patch.shape[0], w_patch.shape[3]
    n_head, hd = w_qkv.shape[2:]
    n_chip = n_dev // 2
    grid_rows = height // patch
    band = pos_embed.shape[0]
    slab = -(-chan * patch // 16) * 16
    select = np.zeros((grid_rows * slab, chan * height), np.float32)
    for y in range(grid_rows):
        for c in range(chan):
            for p in range(patch):
                select[y * slab + c * patch + p, c * height + y * patch + p] = 1.0
    depth = patch * slab
    keys = band * n_dev
    scale = hd ** -0.5 * math.log2(math.e)
    heads_b, heads_a = n_head // 4, n_head // 2
    blk = 2 * band

    def unit(heads):
        return [pltpu.VMEM((heads, hd, keys), BF16), pltpu.VMEM((heads, keys, hd), BF16), pltpu.VMEM((heads, hd, keys), BF16)]

    vmem = pl.BlockSpec(memory_space=pltpu.VMEM)
    hbm = pl.BlockSpec(memory_space=pl.ANY)
    dma = pltpu.SemaphoreType.DMA
    return pl.pallas_call(
        functools.partial(front_kernel, (patch, n_dev, scale)),
        out_shape=[jax.ShapeDtypeStruct((n_img, band, dim), BF16), jax.ShapeDtypeStruct((n_img, n_head, hd, band), BF16)],
        in_specs=[hbm] * 4 + [vmem] * 5,
        out_specs=[vmem, hbm],
        scratch_shapes=[
            pltpu.VMEM((n_img, chan, height, width), F32), pltpu.VMEM((patch, chan, patch, dim), BF16),
            pltpu.VMEM((band, dim), BF16),
            pltpu.VMEM((dim // 128, depth, 128), F32), pltpu.VMEM((depth, dim), BF16), pltpu.VMEM((width, width), BF16),
            pltpu.VMEM((n_img, band, dim), BF16),
            pltpu.VMEM((n_chip, 2, band, dim), BF16), pltpu.VMEM((n_chip, 2, band, dim), BF16),
            pltpu.VMEM((3, heads_b * hd, dim), BF16), pltpu.VMEM((3, heads_a * hd, dim), BF16),
            *unit(heads_b), *unit(heads_a),
            pltpu.VMEM((2, keys, blk), F32), pltpu.VMEM((2, 8, blk), F32),
            pltpu.VMEM((2, keys, blk), BF16), pltpu.VMEM((2, 8, blk), F32),
            pltpu.VMEM((n_chip, 2, heads_b, hd, band), BF16), pltpu.VMEM((n_chip, 2, heads_a, hd, band), BF16),
            dma((n_img,)), dma((2,)), dma((2, 3)), dma((2, n_chip)), dma((2, n_chip)), dma((2, n_chip)), dma((2, n_chip)),
            dma((2, n_chip, 2)), dma((2, n_chip, 2)),
        ],
        compiler_params=pltpu.CompilerParams(collective_id=0, has_side_effects=True, vmem_limit_bytes=60 * 2**20),
        name='front',
    )(jnp.transpose(images, (0, 3, 1, 2)), jnp.transpose(w_patch, (0, 2, 1, 3)),
      jnp.transpose(w_qkv, (1, 2, 3, 0)).reshape(3 * dim, dim), pos_embed, jnp.asarray(select, BF16),
      b_patch, ln1_gain, ln1_bias, b_qkv)


def mlp_kernel(chunk, tail, o_ref, x_ref, wo_ref, bo_ref, g2_ref, c2_ref, b1_ref, b2_ref, w1_hbm, w2_hbm, out_ref,
               w1, w2, acc, y2, hid, sem1, sem2):
    n_full = (w1.shape[0] - tail) // chunk

    def w_copy(i, size):
        rows = pl.ds(i * chunk, size) if isinstance(i, int) else pl.ds(pl.multiple_of(i * chunk, chunk), size)
        return (pltpu.make_async_copy(w1_hbm.at[rows], w1.at[rows], sem1.at[i]),
                pltpu.make_async_copy(w2_hbm.at[rows], w2.at[rows], sem2.at[i]))

    for i in range(n_full + 1):
        for c in w_copy(i, chunk if i < n_full else tail):
            c.start()
    n_img, dim, band = o_ref.shape

    def proj(i, carry):
        rows = pl.ds(pl.multiple_of(i * band, band), band)
        r = lax.dot_general(o_ref[i], wo_ref[...], (((0,), (0,)), ((), ())), preferred_element_type=F32)
        r = x_ref[rows].astype(F32) + r + bo_ref[...].reshape(1, dim)
        acc[rows] = r + b2_ref[...].reshape(1, dim)
        y2[rows] = layer_norm(r, g2_ref[...].reshape(1, dim), c2_ref[...].reshape(1, dim)).astype(BF16)
        return carry

    lax.fori_loop(0, n_img, proj, 0)

    def first(i, size, slot):
        rows = pl.ds(i * chunk, size) if isinstance(i, int) else pl.ds(pl.multiple_of(i * chunk, chunk), size)
        pre = lax.dot_general(y2[...], w1[rows], (((1,), (1,)), ((), ())), preferred_element_type=F32)
        pre = pre + b1_ref[:, rows]
        hid[slot, :, :size] = jax.nn.gelu(pre, approximate=True).astype(BF16)

    def second(i, size, slot):
        rows = pl.ds(i * chunk, size) if isinstance(i, int) else pl.ds(pl.multiple_of(i * chunk, chunk), size)
        acc[...] += jnp.dot(hid[slot, :, :size], w2[rows], preferred_element_type=F32)

    w_copy(0, chunk)[0].wait()
    first(0, chunk, 0)

    def body(i, carry):
        w_copy(i + 1, chunk)[0].wait()
        w_copy(i, chunk)[1].wait()
        first(i + 1, chunk, lax.rem(i + 1, 2))
        second(i, chunk, lax.rem(i, 2))
        return carry

    lax.fori_loop(0, n_full - 1, body, 0)
    w_copy(n_full, tail)[0].wait()
    w_copy(n_full - 1, chunk)[1].wait()
    first(n_full, tail, n_full % 2)
    second(n_full - 1, chunk, (n_full - 1) % 2)
    w_copy(n_full, tail)[1].wait()
    second(n_full, tail, n_full % 2)
    out_ref[...] = acc[...].astype(BF16)


def mlp_layer(o_t, x_zero, w_out, b_out, ln2_gain, ln2_bias, w_fc1_t, b_fc1, w_fc2, b_fc2):
    images, dim, band = o_t.shape
    ff = w_fc2.shape[0]
    rows = images * band
    chunk = 512
    tail = ff - (ff - 1) // chunk * chunk
    n_chunks = (ff - tail) // chunk + 1
    vmem = pl.BlockSpec(memory_space=pltpu.VMEM)
    hbm = pl.BlockSpec(memory_space=pl.ANY)
    flops = 2 * rows * dim * (dim + 2 * ff)
    return pl.pallas_call(
        functools.partial(mlp_kernel, chunk, tail),
        out_shape=jax.ShapeDtypeStruct((rows, dim), BF16),
        in_specs=[vmem] * 8 + [hbm, hbm],
        out_specs=vmem,
        scratch_shapes=[
            pltpu.VMEM((ff, dim), BF16), pltpu.VMEM((ff, dim), BF16), pltpu.VMEM((rows, dim), F32),
            pltpu.VMEM((rows, dim), BF16), pltpu.VMEM((2, rows, chunk), BF16),
            pltpu.SemaphoreType.DMA((n_chunks,)), pltpu.SemaphoreType.DMA((n_chunks,)),
        ],
        compiler_params=pltpu.CompilerParams(vmem_limit_bytes=56 * 2**20),
        cost_estimate=pl.CostEstimate(flops=flops, bytes_accessed=32 * 2**20, transcendentals=0),
        name='mlp',
    )(o_t, x_zero, w_out, b_out, ln2_gain, ln2_bias, b_fc1[None], b_fc2, w_fc1_t, w_fc2)


def solution(mesh):
    n_dev = mesh.shape['sp']

    def device_step(images, w_patch, b_patch, pos_embed, ln1_gain, ln1_bias, w_qkv, b_qkv, w_out, b_out, ln2_gain, ln2_bias, w_fc1, b_fc1, w_fc2, b_fc2):
        dim, _, num_heads, head_dim = w_qkv.shape
        x_zero, o_t = front_layer(images, w_patch, b_patch, pos_embed, ln1_gain, ln1_bias, w_qkv, b_qkv, n_dev)
        num_images, band = x_zero.shape[:2]
        out = mlp_layer(o_t.reshape(num_images, dim, band), x_zero.reshape(num_images * band, dim), w_out.reshape(dim, dim),
                        b_out, ln2_gain, ln2_bias, w_fc1.T, b_fc1, w_fc2, b_fc2)
        return out.reshape(num_images, band, dim)

    in_specs = (P('dp', 'sp', None, None), P(), P(), P('sp', None), P(), P(), P(), P(), P(), P(), P(), P(), P(), P(), P(), P())
    return jax.shard_map(device_step, mesh=mesh, in_specs=in_specs, out_specs=P('dp', 'sp', None), check_vma=False)
```

time: 424 us -> 104 us (0.25); the launches traced: 417 us -> 104 us
  matrix products: 146 us -> 0 us
  waiting for transfers between devices: 137 us -> 0 us
  Pallas kernels: 0 us -> 102 us
  local copies, waits for them, and re-layouts: 89.4 us -> 1.34 us
  other arithmetic: 18.7 us -> 0 us
  between operations: 13.8 us -> 0.17 us
  loops' own time: 12.4 us -> 0 us
    dot_general x16 -> x0, matrix products: 146 us -> none  [the longest x6 66.5 us: one_group(): jnp.einsum('hqk,khe->qhe', att_weights, v_img, preferred_element_type=jnp...]
    all_gather x1 -> x0, waiting for transfers between devices: 137 us -> none  [device_step(): key_value = lax.all_gather(qkv_proj[:, :, 1:], 'sp', axis=1, tiled=True)]
    pallas_call x0 -> x2, Pallas kernels: none -> 102 us  [the longest x1 70.7 us: front_layer(): pl.pallas_call(functools.partial(front_kernel, (patch, n_dev, scale)), ou...]
    squeeze x2 -> x0, local copies, waits for them, and re-layouts: 23.6 us -> none  [device_step(): attended = attend(qkv_proj[:, :, 0], key_value[:, :, 0], key_value[:, :, 1])]
    reshape x1 -> x0, local copies, waits for them, and re-layouts: 21.5 us -> none  [embed_tokens(): images.astype(jnp.bfloat16)]
    while x12 -> x0, local copies, waits for them, and re-layouts: 19.3 us -> none
    dot_general x2 -> x0, local copies, waits for them, and re-layouts: 18.1 us -> none  [embed_tokens(): jnp.einsum('bypxqc,pqcd->byxd', pixels, w_patch, preferred_element_type=j...]
    sub x6 -> x0, other arithmetic: 13.7 us -> none  [one_group(): att_weights = jax.nn.softmax(scores, axis=-1).astype(jnp.bfloat16)]
  transfers between devices with their start and end apart: 1 -> 0, of which waited for: 1 -> 0; matrix products, arithmetic and copies ran while one was open for 1% -> 0% of each run, Pallas kernels for 0% -> 0%
where the time goes in v3:
time: 104 us
  Pallas kernels  102 us (98%)
  local copies, waits for them, and re-layouts  1.34 us (1%)
    pallas_call x1, Pallas kernels, front_layer(): pl.pallas_call(functools.partial(front_kernel, (patch, n_dev, scale)), ou...  70.7 us
    pallas_call x1, Pallas kernels, mlp_layer(): pl.pallas_call(functools.partial(mlp_kernel, chunk, tail), out_shape=jax....  31.5 us

profile of v3, /device:TPU:113, one launch (start us, length us, event | category | flops | bytes accessed | tf_op | source)
XLA Modules:
  0.0 103.7 jit_solution(2439926459560462768)
XLA Ops:
  0.0 1.3 %broadcast_in_dim.3.b1_ref = f32[1,4304]{1,0:T(1,128)} reshape(f32[4304]{0:T(1024)} %param.30) | data formatting | bytes 34432 | tf_op jit(solution)/shard_map/broadcast_in_dim | solution.py:428
  1.3 70.7 %front.1 = (bf16[6,128,1152]{2,1,0:T(8,128)(2,1)}, bf16[6,16,72,128]{3,2,1,0:T(8,128)(2,1)}) custom-call(f32[6,3,56,448]{3,2,1,0:T(8,128)} %bitcast.11, bf16[14,3,14,1152]{3,2,1,0:T(8,128)(2,1)} %bitcast.12, bf16[3456,1152]{1,0:T(8,128)(2,1)} %bitcast.10, bf16[128,1152]{1,0:T(8,128)(2,1)} %pos_hbm.1, bf16[192,168]{1,0:T(8,128)(2,1)} %constant.2.clone.sel_ref, ...), custom_call_target="tpu_custom_call" | custom-call | tf_op jit(solution)/shard_map/front/pallas_call | solution.py:325
  72.0 31.5 %mlp.1 = bf16[768,1152]{1,0:T(8,128)(2,1)} custom-call(bf16[6,1152,128]{2,1,0:T(8,128)(2,1)} %bitcast.16, bf16[768,1152]{1,0:T(8,128)(2,1)} %bitcast.15, bf16[1152,1152]{1,0:T(8,128)(2,1)} %bitcast.14, f32[1152]{0:T(1024)} %bo_ref.1, f32[1152]{0:T(1024)} %g2_ref.1, f32[1152]{0:T(1024)} %c2_ref.1, f32[1,4304]{1,0:T(1,128)} %broadcast_in_dim.3.b1_ref, ...), custom_call_target="tpu_custom_call" | custom-call | flops 17270046720 | bytes 33554432 | tf_op jit(solution)/shard_map/mlp/pallas_call | solution.py:415
